TPU v7x, 128 devices: a whole 4x4x4 slice. The times are simulated.
128 devices in a mesh: attn: 4 (over x), expert: 32 (over z, y, core).
Axes of the slice: x: 4, y: 4, z: 4, core: 2. Of those that a mesh axis runs over, the one named last changes fastest.
Arguments:
- tokens: bfloat16 [4096, 2880], P(('attn', 'expert')), may hold values from -6 to 6
- expert_ids: int32 [4096, 4], P(('attn', 'expert')), may hold values from 0 to 31, all different within a row; in each aligned block of 32 rows (0 to 31, 32 to 63, ...) at most 12 rows name the same one
- gate_probs: float32 [4096, 4], P(('attn', 'expert')), may hold values from 0.05 to 0.6
- shed_blocks: int32 [32], replicated, may hold values from 0 to 4, as said below
- partner: int32 [32], replicated, may hold values from 0 to 31, as said below
- gate_weight: bfloat16 [32, 2880, 2880], P('expert', None, 'attn'), may hold values from -0.109375 to 0.109375
- up_weight: bfloat16 [32, 2880, 2880], P('expert', None, 'attn'), may hold values from -0.109375 to 0.109375
- down_weight: bfloat16 [32, 2880, 2880], P('expert', 'attn'), may hold values from -0.109375 to 0.109375
Outputs:
- moe_out: bfloat16 [4096, 2880], P(('attn', 'expert'))
Inputs may be any that keep to these rules, and one draw needn't show every extreme that they name: `expert_ids`: in the rows of one device, no expert is named by more than 12 rows; the 4 experts of a token differ. `shed_blocks`: some expert has exactly 4. partner pairs the experts: partner[partner[e]] = e and partner[e] != e.
All inputs are finite; a program needn't handle non-finite values.
Results may differ from a plain program's by a relative error of at most 0.0081.
Values may be sent and summed in bfloat16 or wider, within the bound.
No kernel may reach another device: no remote copies, remote signals or barrier semaphores. Data moves between devices by JAX's collectives and lax.ppermute only.
A program may use at most 128 MiB of HBM per device.

v0:
```python
import jax
import jax.numpy as jnp
from jax import lax
from jax.sharding import Mesh
from jax.sharding import PartitionSpec as P

SHED_MOST = 4
ATTN_EXPERT = ("attn", "expert_0", "expert_1", "expert_2")
EXPERT = ("expert_0", "expert_1", "expert_2")
SWISH_SCALE = 1.702


def nothing_yet(array, identity):
    return jnp.broadcast_to(jnp.asarray(identity, array.dtype), array.shape)


def prefix_by_axis(array, axes, combine, identity):
    before = start = nothing_yet(array, identity)
    total = array
    for axis in reversed(axes):
        devices, mine = (lax.axis_size(axis), lax.axis_index(axis))
        pieces = lax.all_gather(total, axis)
        inside, total = (start, start)
        for k in range(devices):
            passed = k < mine
            total = combine(total, pieces[k])
            inside = jnp.where(passed, total, inside)
        before = combine(inside, before)
    return before


def split_up(array, dim, devices):
    dims = array.shape
    parts = array.reshape(*dims[:dim], devices, dims[dim] // devices, *dims[dim + 1 :])
    return jnp.moveaxis(parts, dim, 0)


def sum_at_owner(array, axis, dim):
    parts = split_up(array, dim, lax.axis_size(axis))
    arrived = lax.all_to_all(parts, axis, split_axis=0, concat_axis=0, tiled=True)
    return arrived.astype(jnp.float32).sum(axis=0)


def lookup(table, indices):
    places = jnp.arange(table.shape[0], dtype=jnp.int32)
    return jnp.sum(jnp.where(indices[:, None] == places[None, :], table[None, :], 0), axis=1)


def add_counts(earlier, later):
    return earlier + later


def activate(rows, gate_w, up_w):
    gate_part = jnp.dot(rows, gate_w, preferred_element_type=jnp.float32)
    up_part = jnp.dot(rows, up_w, preferred_element_type=jnp.float32)
    return (gate_part * jax.nn.sigmoid(SWISH_SCALE * gate_part) * (up_part + 1.0)).astype(
        jnp.bfloat16
    )


def on_device(
    tokens, expert_ids, gate_probs, shed_blocks, partner, gate_weight, up_weight, down_weight
):
    tok_rows, model_width = tokens.shape
    top_count = expert_ids.shape[1]
    expert_count = shed_blocks.shape[0]
    group_count = lax.axis_size("attn")
    capacity = tok_rows * top_count * group_count
    block_size = capacity // 8
    most_rows = min(tok_rows, 3 * tok_rows * top_count // expert_count)
    slot_count = 2 * most_rows
    places = jnp.arange(expert_count, dtype=jnp.int32)
    flat_ids = expert_ids.reshape(-1)
    onehot = (flat_ids[:, None] == places[None, :]).astype(jnp.int32)
    counts = jnp.sum(onehot, axis=0)
    local_rank = jnp.sum((jnp.cumsum(onehot, axis=0) - onehot) * onehot, axis=1)
    offsets = prefix_by_axis(counts, ATTN_EXPERT, add_counts, jnp.zeros_like(counts))
    global_rank = local_rank + jnp.sum(onehot * offsets[None, :], axis=1)
    limit = capacity - block_size * lookup(shed_blocks, partner)
    own_limit = lookup(limit, flat_ids)
    own_shed = lookup(shed_blocks, flat_ids)
    native = global_rank < own_limit
    borrowed = jnp.logical_and(
        jnp.logical_not(native), global_rank < own_limit + block_size * own_shed
    )
    usable = jnp.logical_or(native, borrowed)
    target = jnp.where(usable, flat_ids, -1)
    table_rows = capacity + block_size * SHED_MOST
    target_hot = (target[:, None] == places[None, :]).astype(jnp.int32)
    position = jnp.sum((jnp.cumsum(target_hot, axis=0) - target_hot) * target_hot, axis=1)
    buffer_index = jnp.where(usable, target * slot_count + position, expert_count * slot_count)
    token_rows = jnp.repeat(tokens, top_count, axis=0)
    send_rows = (
        jnp.zeros((expert_count * slot_count, model_width), jnp.bfloat16)
        .at[buffer_index]
        .set(token_rows, mode="drop")
    )
    send_slots = (
        jnp.full((expert_count * slot_count,), table_rows, jnp.int32)
        .at[buffer_index]
        .set(global_rank, mode="drop")
    )
    send_rows = send_rows.reshape(expert_count, slot_count, model_width)
    send_slots = send_slots.reshape(expert_count, slot_count)
    got_rows, got_slots = (
        lax.all_to_all(send_rows, EXPERT, split_axis=0, concat_axis=0, tiled=True),
        lax.all_to_all(send_slots, EXPERT, split_axis=0, concat_axis=0, tiled=True),
    )
    local_table = (
        jnp.zeros((table_rows, model_width), jnp.float32)
        .at[got_slots.reshape(-1)]
        .set(got_rows.reshape(-1, model_width).astype(jnp.float32), mode="drop")
    )
    compact = lax.psum(local_table.astype(jnp.bfloat16), "attn")
    gate_own = gate_weight[0]
    up_own = up_weight[0]
    down_own = down_weight[0]
    hidden_own = activate(compact, gate_own, up_own)
    share = sum_at_owner(
        jnp.dot(hidden_own, down_own, preferred_element_type=jnp.float32).astype(jnp.bfloat16),
        "attn",
        0,
    )
    results = lax.all_gather(share.astype(jnp.bfloat16), "attn", axis=0, tiled=True)
    answers = results[jnp.minimum(got_slots, table_rows - 1)]
    returned = lax.all_to_all(answers, EXPERT, split_axis=0, concat_axis=0, tiled=True)
    flat_back = returned.reshape(expert_count * slot_count, model_width)
    picked = flat_back[jnp.minimum(buffer_index, expert_count * slot_count - 1)]
    weights = jnp.where(usable, gate_probs.reshape(-1), 0.0)
    mixed = picked.astype(jnp.float32) * weights[:, None]
    return mixed.reshape(tok_rows, top_count, model_width).sum(axis=1).astype(jnp.bfloat16)


def solution(mesh):
    split = Mesh(
        mesh.devices.reshape(mesh.shape["attn"], 4, 4, 2),
        ("attn", "expert_0", "expert_1", "expert_2"),
    )
    return jax.shard_map(
        on_device,
        mesh=split,
        in_specs=(
            P(ATTN_EXPERT, None),
            P(ATTN_EXPERT, None),
            P(ATTN_EXPERT, None),
            P(),
            P(),
            P(EXPERT, None, "attn"),
            P(EXPERT, None, "attn"),
            P(EXPERT, "attn", None),
        ),
        out_specs=P(ATTN_EXPERT, None),
        check_vma=False,
    )
```

profile of v0, /device:TPU:0, one launch (start us, length us, event | category | flops | bytes accessed | tf_op | source)
XLA Modules:
  0.0 470.4 jit_solution(2602426872722942839)
XLA Ops:
  7.7 1.2 dynamic-slice
  9.9 1.8 all-reduce
  13.7 9.2 %all-reduce.1 = s32[128]{0:T(128)S(1)} all-reduce(s32[128]{0:T(128)S(1)} %fusion.33), channel_id=3, replica_groups=mesh['attn'=4,'expert_0'=4,'expert_1'=4,'expert_2'=2] {'expert_1'}, use_global_device_ids=true, to_apply=%add.1 | all-reduce | flops 128 | bytes 1024
  23.0 11.0 %all-gather.2 = s32[4,1,32]{2,1,0:T(1,128)S(1)} all-gather(s32[1,1,32]{2,1,0:T(1,128)S(1)} %fusion.37), channel_id=1, replica_groups=mesh['attn'=4,'expert_0'=4,'expert_1'=4,'expert_2'=2] {'expert_0'}, dimensions={0}, use_global_device_ids=true | all-gather | bytes 640 | tf_op jit(solution)/shard_map/all_gather | solution.py:22
  34.0 9.7 %all-gather.3 = s32[4,1,32]{2,1,0:T(1,128)S(1)} all-gather(s32[1,1,32]{2,1,0:T(1,128)S(1)} %slice_add_fusion.3), channel_id=1, replica_groups=mesh['attn'=4,'expert_0'=4,'expert_1'=4,'expert_2'=2] {'attn'}, dimensions={0}, use_global_device_ids=true | all-gather | bytes 640 | tf_op jit(solution)/shard_map/all_gather | solution.py:22
  47.9 3.8 all-to-all-start
  53.2 4.6 scatter_custom_fusion.1
  57.7 1.3 all-to-all-done
  59.0 6.2 %all-to-all-start.1 = ((bf16[32,24,2880]{2,1,0:T(8,128)(2,1)}), bf16[32,24,2880]{2,1,0:T(8,128)(2,1)}, u32[]{:S(2)}, u32[]{:S(2)}) async-start(bf16[32,24,2880]{2,1,0:T(8,128)(2,1)} %bitcast.70), calls=%async_computation.1 | async-start | bytes 9043968 | tf_op jit(solution)/shard_map/all_to_all | solution.py:106
  66.8 56.1 %all-to-all-done.1 = bf16[32,24,2880]{2,1,0:T(8,128)(2,1)} async-done(((bf16[32,24,2880]{2,1,0:T(8,128)(2,1)}), bf16[32,24,2880]{2,1,0:T(8,128)(2,1)}, u32[]{:S(2)}, u32[]{:S(2)}) %all-to-all-start.1) | async-done | bytes 4423712 | tf_op jit(solution)/shard_map/all_to_all | solution.py:106
  122.9 13.9 %scatter_custom_fusion.2 = f32[768,2880]{1,0:T(8,128)} fusion(s32[768]{0:T(1024)S(1)} %fusion.20, bf16[768,2880]{1,0:T(8,128)(2,1)} %bitcast.25, f32[]{:T(128)} %constant.17.clone.1), kind=kCustom, calls=%fused_computation.5 | custom fusion | flops 2211840 | bytes 13271044 | tf_op jit(solution)/shard_map/scatter | solution.py:112
  136.8 6.2 %convert_element_type.37 = bf16[768,2880]{1,0:T(8,128)(2,1)} convert(f32[768,2880]{1,0:T(8,128)} %scatter_custom_fusion.2) | non-fusion elementwise | flops 2211840 | bytes 13271040 | tf_op jit(solution)/shard_map/convert_element_type | solution.py:114
  143.3 92.2 %all-reduce.4.cloned.1.call-done = bf16[768,2880]{1,0:T(8,128)(2,1)} async-done(((bf16[768,2880]{1,0:T(8,128)(2,1)}), bf16[768,2880]{1,0:T(8,128)(2,1)}) %all-reduce.4.cloned.1.call-update) | async-done | bytes 4423696 | tf_op jit(solution)/shard_map/psum | solution.py:114
  235.5 8.6 %fusion.4 = f32[768,720]{0,1:T(8,128)} fusion(bf16[768,2880]{1,0:T(8,128)(2,1)} %all-reduce.4.cloned.1.call-done, bf16[1,2880,720]{1,2,0:T(8,128)(2,1)} %param.14), kind=kOutput, calls=%fused_computation.10 | convolution fusion | flops 3185049600 | bytes 10782720 | tf_op jit(solution)/shard_map/dot_general | solution.py:55
  244.1 15.6 %convolution_convert_fusion = bf16[768,2880]{0,1:T(8,128)(2,1)} fusion(bf16[1,720,2880]{2,1,0:T(8,128)(2,1)} %param.15, f32[768,720]{0,1:T(8,128)} %fusion.4, bf16[768,2880]{1,0:T(8,128)(2,1)} %all-reduce.4.cloned.1.call-done, bf16[1,2880,720]{1,2,0:T(8,128)(2,1)} %param.13), kind=kOutput, calls=%fused_computation.7 | convolution fusion | flops 6376734720 | bytes 19353600 | tf_op jit(solution)/shard_map/dot_general | solution.py:120
  259.7 6.5 %copy.24 = bf16[768,2880]{1,0:T(8,128)(2,1)} copy(bf16[768,2880]{0,1:T(8,128)(2,1)} %convolution_convert_fusion) | data formatting | bytes 8847360 | tf_op jit(solution)/shard_map/convert_element_type | solution.py:120
  266.2 58.4 %all_to_all.24 = bf16[4,192,2880]{2,1,0:T(8,128)(2,1)} all-to-all(bf16[4,192,2880]{2,1,0:T(8,128)(2,1)} %bitcast.71), channel_id=1, replica_groups=mesh['attn'=4,'expert_0'=4,'expert_1'=4,'expert_2'=2] {'attn'}, dimensions={0} | all-to-all | bytes 8847360 | tf_op jit(solution)/shard_map/all_to_all | solution.py:40
  324.6 4.3 reduce_sum.99
  329.0 50.4 %all-gather.6.cloned.1.call-done = bf16[768,2880]{1,0:T(8,128)(2,1)} async-done(((bf16[192,2880]{1,0:T(8,128)(2,1)}), bf16[768,2880]{1,0:T(8,128)(2,1)}) %all-gather.6.cloned.1.call-update) | async-done | bytes 4423696 | tf_op jit(solution)/shard_map/all_gather | solution.py:124
  379.4 12.2 %gather_fusion = bf16[768,2880]{1,0:T(8,128)(2,1)} fusion(bf16[768,2880]{1,0:T(8,128)(2,1)} %all-gather.6.cloned.1.call-done, s32[1024]{0:T(1024)S(1)} %pad_clamp_fusion.1), kind=kCustom, calls=%fused_computation | custom fusion | bytes 8850432 | tf_op jit(solution)/shard_map/gather | solution.py:125
  391.7 7.5 %all-to-all-start.3 = ((bf16[32,24,2880]{2,1,0:T(8,128)(2,1)}), bf16[32,24,2880]{2,1,0:T(8,128)(2,1)}, u32[]{:S(2)}, u32[]{:S(2)}) async-start(bf16[32,24,2880]{2,1,0:T(8,128)(2,1)} %bitcast.69), calls=%async_computation.3 | async-start | bytes 9043968 | tf_op jit(solution)/shard_map/all_to_all | solution.py:126
  399.6 57.2 %all-to-all-done.3 = bf16[32,24,2880]{2,1,0:T(8,128)(2,1)} async-done(((bf16[32,24,2880]{2,1,0:T(8,128)(2,1)}), bf16[32,24,2880]{2,1,0:T(8,128)(2,1)}, u32[]{:S(2)}, u32[]{:S(2)}) %all-to-all-start.3) | async-done | bytes 4423712 | tf_op jit(solution)/shard_map/all_to_all | solution.py:126
  456.8 4.7 gather_fusion.1
  461.9 1.7 multiply_reduce_fusion
  (47 shorter events, 11.2 us)
Async XLA Ops:
  47.9 11.1 %all-to-all-start = ((s32[32,1,24]{2,1,0:T(1,128)}), s32[32,1,24]{2,1,0:T(1,128)S(1)}, u32[]{:S(2)}, u32[]{:S(2)}) async-start(s32[32,1,24]{2,1,0:T(1,128)} %bitcast.14), calls=%async_computation | async-start | bytes 32768 | tf_op jit(solution)/shard_map/all_to_all | solution.py:107
  59.0 63.9 %all-to-all-start.1 = ((bf16[32,24,2880]{2,1,0:T(8,128)(2,1)}), bf16[32,24,2880]{2,1,0:T(8,128)(2,1)}, u32[]{:S(2)}, u32[]{:S(2)}) async-start(bf16[32,24,2880]{2,1,0:T(8,128)(2,1)} %bitcast.70), calls=%async_computation.1 | async-start | bytes 9043968 | tf_op jit(solution)/shard_map/all_to_all | solution.py:106
  65.2 170.3 %all-reduce.4.cloned.1.call-start = ((), (), s32[]{:S(2)}) async-start(), calls=%async_computation.4 | async-start | bytes 9043968 | tf_op jit(solution)/shard_map/psum | solution.py:114
  143.0 236.4 %all-gather.6.cloned.1.call-start = ((), (), s32[]{:S(2)}) async-start(), calls=%async_computation.5 | async-start | bytes 5652480 | tf_op jit(solution)/shard_map/all_gather | solution.py:124
  391.6 7.8 %copy-start = (f32[32,4]{0,1:T(4,128)S(1)}, f32[32,4]{0,1:T(4,128)}, u32[]{:S(2)}) copy-start(f32[32,4]{0,1:T(4,128)} %param.10) | copy-start | bytes 1540
  391.7 65.2 %all-to-all-start.3 = ((bf16[32,24,2880]{2,1,0:T(8,128)(2,1)}), bf16[32,24,2880]{2,1,0:T(8,128)(2,1)}, u32[]{:S(2)}, u32[]{:S(2)}) async-start(bf16[32,24,2880]{2,1,0:T(8,128)(2,1)} %bitcast.69), calls=%async_computation.3 | async-start | bytes 9043968 | tf_op jit(solution)/shard_map/all_to_all | solution.py:126
Sparse Core Ops, SparseCore 0:
  143.2 92.3 all-reduce.3
  329.0 50.3 all-gather.5
where the time goes:
time: 471 us; the launch traced here: 470 us
  waiting for transfers between devices  257 us (55%)
  blocking collectives  90.1 us (19%)
  local copies, waits for them, and re-layouts  36.3 us (8%)
  other arithmetic  29.7 us (6%)
  matrix products  24.2 us (5%)
  starting transfers between devices  18.1 us (4%)
  between operations  14.9 us (3%)
    psum x1, waiting for transfers between devices, on_device(): compact = lax.psum(local_table.astype(jnp.bfloat16), 'attn')  92.2 us
    all_to_all x1, blocking collectives, sum_at_owner(): lax.all_to_all(parts, axis, split_axis=0, concat_axis=0, tiled=True)  58.4 us
    all_to_all x1, waiting for transfers between devices, on_device(): lax.all_to_all(answers, EXPERT, split_axis=0, concat_axis=0, tiled=True)  57.2 us
    all_to_all x1, waiting for transfers between devices, on_device(): lax.all_to_all(send_rows, EXPERT, split_axis=0, concat_axis=0, tiled=True)  56.1 us
    all_gather x1, waiting for transfers between devices, on_device(): lax.all_gather(share.astype(jnp.bfloat16), 'attn', axis=0, tiled=True)  50.4 us
    all_gather x2, blocking collectives, prefix_by_axis(): pieces = lax.all_gather(total, axis)  20.7 us
    dot_general x1, matrix products, on_device(): jnp.dot(hidden_own, down_own, preferred_element_type=jnp.float32)  15.6 us
    scatter x1, other arithmetic, on_device(): local_table = jnp.zeros((table_rows, model_width), jnp.float32).at[got_sl...  13.9 us
  transfers between devices with their start and end apart: 5, of which 5 were waited for; matrix products, arithmetic and copies ran while one was open for 2% of the time, Pallas kernels for 0%

commit v1 on v0

--- a/solution.py
+++ b/solution.py
@@ -8,6 +8,27 @@
 ATTN_EXPERT = ("attn", "expert_0", "expert_1", "expert_2")
 EXPERT = ("expert_0", "expert_1", "expert_2")
 SWISH_SCALE = 1.702
+
+
+def gather_around(array, axis, dim):
+    length, index, width = (lax.axis_size(axis), lax.axis_index(axis), array.shape[dim])
+    right = [(i, (i + 1) % length) for i in range(length)]
+    behind = [(i, (i - 1) % length) for i in range(length)]
+    result = jnp.zeros((*array.shape[:dim], length * width, *array.shape[dim + 1 :]), array.dtype)
+    result = lax.dynamic_update_slice_in_dim(result, array, index * width, axis=dim)
+    from_left = from_right = array
+    middle = length // 2
+    for hop in range(1, middle + 1):
+        from_left = lax.ppermute(from_left, axis, right)
+        result = lax.dynamic_update_slice_in_dim(
+            result, from_left, (index - hop) % length * width, axis=dim
+        )
+        if hop < length - middle:
+            from_right = lax.ppermute(from_right, axis, behind)
+            result = lax.dynamic_update_slice_in_dim(
+                result, from_right, (index + hop) % length * width, axis=dim
+            )
+    return result
 
 
 def nothing_yet(array, identity):
@@ -121,7 +142,7 @@
         "attn",
         0,
     )
-    results = lax.all_gather(share.astype(jnp.bfloat16), "attn", axis=0, tiled=True)
+    results = gather_around(share.astype(jnp.bfloat16), "attn", 0)
     answers = results[jnp.minimum(got_slots, table_rows - 1)]
     returned = lax.all_to_all(answers, EXPERT, split_axis=0, concat_axis=0, tiled=True)
     flat_back = returned.reshape(expert_count * slot_count, model_width)

time: 471 us -> 471 us (level)
  local copies, waits for them, and re-layouts: 36.3 us -> 43.1 us
  waiting for transfers between devices: 257 us -> 251 us
    all_gather x1 -> x0, waiting for transfers between devices: 50.4 us -> none  [on_device(): lax.all_gather(share.astype(jnp.bfloat16), 'attn', axis=0, tiled=True)]
    ppermute x0 -> x3, waiting for transfers between devices: none -> 43.6 us  [the longest x2 43.6 us: gather_around(): from_left = lax.ppermute(from_left, axis, right)]
  transfers between devices with their start and end apart: 5 -> 7, of which waited for: 5 -> 6; matrix products, arithmetic and copies ran while one was open for 2% -> 3% of each run, Pallas kernels for 0% -> 0%
where the time goes in v1:
time: 471 us
  waiting for transfers between devices  251 us (53%)
  blocking collectives  90.1 us (19%)
  local copies, waits for them, and re-layouts  43.1 us (9%)
  other arithmetic  28.9 us (6%)
  matrix products  21.7 us (5%)
  starting transfers between devices  21.1 us (4%)
  between operations  14.9 us (3%)
    psum x1, waiting for transfers between devices, on_device(): compact = lax.psum(local_table.astype(jnp.bfloat16), 'attn')  92.5 us
    all_to_all x1, blocking collectives, sum_at_owner(): lax.all_to_all(parts, axis, split_axis=0, concat_axis=0, tiled=True)  58.4 us
    all_to_all x1, waiting for transfers between devices, on_device(): lax.all_to_all(answers, EXPERT, split_axis=0, concat_axis=0, tiled=True)  57.2 us
    all_to_all x1, waiting for transfers between devices, on_device(): lax.all_to_all(send_rows, EXPERT, split_axis=0, concat_axis=0, tiled=True)  56.1 us
    ppermute x2, waiting for transfers between devices, gather_around(): from_left = lax.ppermute(from_left, axis, right)  43.6 us
    all_gather x2, blocking collectives, prefix_by_axis(): pieces = lax.all_gather(total, axis)  20.7 us
    dot_general x1, matrix products, on_device(): jnp.dot(hidden_own, down_own, preferred_element_type=jnp.float32)  14.9 us
    scatter x1, other arithmetic, on_device(): local_table = jnp.zeros((table_rows, model_width), jnp.float32).at[got_sl...  13.9 us
  transfers between devices with their start and end apart: 7, of which 6 were waited for; matrix products, arithmetic and copies ran while one was open for 3% of the time, Pallas kernels for 0%

profile of v1, /device:TPU:0, one launch (start us, length us, event | category | flops | bytes accessed | tf_op | source)
XLA Modules:
  0.0 470.5 jit_solution(16814677028537731703)
XLA Ops:
  9.9 1.8 all-reduce
  13.7 9.2 %all-reduce.1 = s32[128]{0:T(128)S(1)} all-reduce(s32[128]{0:T(128)S(1)} %fusion.33), channel_id=3, replica_groups=mesh['attn'=4,'expert_0'=4,'expert_1'=4,'expert_2'=2] {'expert_1'}, use_global_device_ids=true, to_apply=%add.1 | all-reduce | flops 128 | bytes 1024
  23.0 11.0 %all-gather.2 = s32[4,1,32]{2,1,0:T(1,128)S(1)} all-gather(s32[1,1,32]{2,1,0:T(1,128)S(1)} %fusion.37), channel_id=1, replica_groups=mesh['attn'=4,'expert_0'=4,'expert_1'=4,'expert_2'=2] {'expert_0'}, dimensions={0}, use_global_device_ids=true | all-gather | bytes 640 | tf_op jit(solution)/shard_map/all_gather | solution.py:43
  34.0 9.7 %all-gather.3 = s32[4,1,32]{2,1,0:T(1,128)S(1)} all-gather(s32[1,1,32]{2,1,0:T(1,128)S(1)} %slice_add_fusion.3), channel_id=1, replica_groups=mesh['attn'=4,'expert_0'=4,'expert_1'=4,'expert_2'=2] {'attn'}, dimensions={0}, use_global_device_ids=true | all-gather | bytes 640 | tf_op jit(solution)/shard_map/all_gather | solution.py:43
  47.9 3.8 all-to-all-start
  53.2 4.6 scatter_custom_fusion.1
  59.0 6.2 %all-to-all-start.1 = ((bf16[32,24,2880]{2,1,0:T(8,128)(2,1)}), bf16[32,24,2880]{2,1,0:T(8,128)(2,1)}, u32[]{:S(2)}, u32[]{:S(2)}) async-start(bf16[32,24,2880]{2,1,0:T(8,128)(2,1)} %bitcast.70), calls=%async_computation.1 | async-start | bytes 9043968 | tf_op jit(solution)/shard_map/all_to_all | solution.py:127
  66.8 56.1 %all-to-all-done.1 = bf16[32,24,2880]{2,1,0:T(8,128)(2,1)} async-done(((bf16[32,24,2880]{2,1,0:T(8,128)(2,1)}), bf16[32,24,2880]{2,1,0:T(8,128)(2,1)}, u32[]{:S(2)}, u32[]{:S(2)}) %all-to-all-start.1) | async-done | bytes 4423712 | tf_op jit(solution)/shard_map/all_to_all | solution.py:127
  122.9 13.9 %scatter_custom_fusion.2 = f32[768,2880]{1,0:T(8,128)} fusion(s32[768]{0:T(1024)S(1)} %fusion.20, bf16[768,2880]{1,0:T(8,128)(2,1)} %bitcast.25, f32[]{:T(128)} %constant.33.clone.1), kind=kCustom, calls=%fused_computation.5 | custom fusion | flops 2211840 | bytes 13271044 | tf_op jit(solution)/shard_map/scatter | solution.py:133
  136.8 6.2 %convert_element_type.37 = bf16[768,2880]{1,0:T(8,128)(2,1)} convert(f32[768,2880]{1,0:T(8,128)} %scatter_custom_fusion.2) | non-fusion elementwise | flops 2211840 | bytes 13271040 | tf_op jit(solution)/shard_map/convert_element_type | solution.py:135
  143.0 92.5 %all-reduce.4.cloned.1.call-done = bf16[768,2880]{1,0:T(8,128)(2,1)} async-done(((bf16[768,2880]{1,0:T(8,128)(2,1)}), bf16[768,2880]{1,0:T(8,128)(2,1)}) %all-reduce.4.cloned.1.call-update) | async-done | bytes 4423696 | tf_op jit(solution)/shard_map/psum | solution.py:135
  235.5 6.8 %fusion.4 = f32[768,720]{0,1:T(8,128)S(1)} fusion(bf16[768,2880]{1,0:T(8,128)(2,1)} %all-reduce.4.cloned.1.call-done, bf16[1,2880,720]{1,2,0:T(8,128)(2,1)} %param.14), kind=kOutput, calls=%fused_computation.10 | convolution fusion | flops 3185049600 | bytes 10782720 | tf_op jit(solution)/shard_map/dot_general | solution.py:76
  242.3 14.9 %convolution_convert_fusion = bf16[768,2880]{0,1:T(8,128)(2,1)} fusion(bf16[1,720,2880]{2,1,0:T(8,128)(2,1)} %param.15, f32[768,720]{0,1:T(8,128)S(1)} %fusion.4, bf16[768,2880]{1,0:T(8,128)(2,1)} %all-reduce.4.cloned.1.call-done, bf16[1,2880,720]{1,2,0:T(8,128)(2,1)} %param.13), kind=kOutput, calls=%fused_computation.7 | convolution fusion | flops 6376734720 | bytes 19353600 | tf_op jit(solution)/shard_map/dot_general | solution.py:141
  257.2 6.5 %copy.24 = bf16[768,2880]{1,0:T(8,128)(2,1)} copy(bf16[768,2880]{0,1:T(8,128)(2,1)} %convolution_convert_fusion) | data formatting | bytes 8847360 | tf_op jit(solution)/shard_map/convert_element_type | solution.py:141
  263.7 58.4 %all_to_all.24 = bf16[4,192,2880]{2,1,0:T(8,128)(2,1)} all-to-all(bf16[4,192,2880]{2,1,0:T(8,128)(2,1)} %bitcast.71), channel_id=1, replica_groups=mesh['attn'=4,'expert_0'=4,'expert_1'=4,'expert_2'=2] {'attn'}, dimensions={0} | all-to-all | bytes 8847360 | tf_op jit(solution)/shard_map/all_to_all | solution.py:61
  322.1 3.5 reduce_sum.99
  326.3 2.7 collective-permute-start.1
  329.0 23.5 %collective-permute-done = bf16[192,2880]{1,0:T(8,128)(2,1)S(1)} collective-permute-done((bf16[192,2880]{1,0:T(8,128)(2,1)S(1)}, bf16[192,2880]{1,0:T(8,128)(2,1)S(1)}, u32[]{:S(2)}, u32[]{:S(2)}) %collective-permute-start) | collective-permute-done | bytes 1105952 | tf_op jit(solution)/shard_map/ppermute | solution.py:22
  352.6 2.4 broadcast.186
  358.4 20.1 %collective-permute-done.2 = bf16[192,2880]{1,0:T(8,128)(2,1)S(1)} collective-permute-done((bf16[192,2880]{1,0:T(8,128)(2,1)S(1)}, bf16[192,2880]{1,0:T(8,128)(2,1)S(1)}, u32[]{:S(2)}, u32[]{:S(2)}) %collective-permute-start.2) | collective-permute-done | bytes 1105952 | tf_op jit(solution)/shard_map/ppermute | solution.py:22
  379.6 12.2 %gather_fusion = bf16[768,2880]{1,0:T(8,128)(2,1)} fusion(bf16[768,2880]{1,0:T(8,128)(2,1)} %constant_dynamic-update-slice_fusion, s32[1024]{0:T(1024)S(1)} %pad_clamp_fusion.1), kind=kCustom, calls=%fused_computation | custom fusion | bytes 8850432 | tf_op jit(solution)/shard_map/gather | solution.py:146
  391.7 7.5 %all-to-all-start.3 = ((bf16[32,24,2880]{2,1,0:T(8,128)(2,1)}), bf16[32,24,2880]{2,1,0:T(8,128)(2,1)}, u32[]{:S(2)}, u32[]{:S(2)}) async-start(bf16[32,24,2880]{2,1,0:T(8,128)(2,1)} %bitcast.69), calls=%async_computation.3 | async-start | bytes 9043968 | tf_op jit(solution)/shard_map/all_to_all | solution.py:147
  399.7 57.2 %all-to-all-done.3 = bf16[32,24,2880]{2,1,0:T(8,128)(2,1)} async-done(((bf16[32,24,2880]{2,1,0:T(8,128)(2,1)}), bf16[32,24,2880]{2,1,0:T(8,128)(2,1)}, u32[]{:S(2)}, u32[]{:S(2)}) %all-to-all-start.3) | async-done | bytes 4423712 | tf_op jit(solution)/shard_map/all_to_all | solution.py:147
  456.9 4.7 gather_fusion.1
  (55 shorter events, 20.2 us)
Async XLA Ops:
  47.9 11.1 %all-to-all-start = ((s32[32,1,24]{2,1,0:T(1,128)}), s32[32,1,24]{2,1,0:T(1,128)S(1)}, u32[]{:S(2)}, u32[]{:S(2)}) async-start(s32[32,1,24]{2,1,0:T(1,128)} %bitcast.14), calls=%async_computation | async-start | bytes 32768 | tf_op jit(solution)/shard_map/all_to_all | solution.py:128
  59.0 63.9 %all-to-all-start.1 = ((bf16[32,24,2880]{2,1,0:T(8,128)(2,1)}), bf16[32,24,2880]{2,1,0:T(8,128)(2,1)}, u32[]{:S(2)}, u32[]{:S(2)}) async-start(bf16[32,24,2880]{2,1,0:T(8,128)(2,1)} %bitcast.70), calls=%async_computation.1 | async-start | bytes 9043968 | tf_op jit(solution)/shard_map/all_to_all | solution.py:127
  65.2 170.3 %all-reduce.4.cloned.1.call-start = ((), (), s32[]{:S(2)}) async-start(), calls=%async_computation.4 | async-start | bytes 9043968 | tf_op jit(solution)/shard_map/psum | solution.py:135
  325.6 26.9 %collective-permute-start = (bf16[192,2880]{1,0:T(8,128)(2,1)S(1)}, bf16[192,2880]{1,0:T(8,128)(2,1)S(1)}, u32[]{:S(2)}, u32[]{:S(2)}) collective-permute-start(bf16[192,2880]{1,0:T(8,128)(2,1)S(1)} %reduce_sum.99), channel_id=1, source_target_pairs={{0,32},{32,64},{64,96},{96,0},{1,33},{33,65},{65,97},{97,1},{2,34}... | collective-permute-start | bytes 3317768 | tf_op jit(solution)/shard_map/ppermute | solution.py:22
  326.3 31.0 %collective-permute-start.1 = (bf16[192,2880]{1,0:T(8,128)(2,1)S(1)}, bf16[192,2880]{1,0:T(8,128)(2,1)S(1)}, u32[]{:S(2)}, u32[]{:S(2)}) collective-permute-start(bf16[192,2880]{1,0:T(8,128)(2,1)S(1)} %reduce_sum.99), channel_id=1, source_target_pairs={{0,96},{32,0},{64,32},{96,64},{1,97},{33,1},{65,33},{97,65},{2,98}... | collective-permute-start | bytes 3317768 | tf_op jit(solution)/shard_map/ppermute | solution.py:27
  352.5 26.0 %collective-permute-start.2 = (bf16[192,2880]{1,0:T(8,128)(2,1)S(1)}, bf16[192,2880]{1,0:T(8,128)(2,1)S(1)}, u32[]{:S(2)}, u32[]{:S(2)}) collective-permute-start(bf16[192,2880]{1,0:T(8,128)(2,1)S(1)} %collective-permute-done), channel_id=1, source_target_pairs={{0,32},{32,64},{64,96},{96,0},{1,33},{33,65},{65,97},{97,1},{2,34}... | collective-permute-start | bytes 3317768 | tf_op jit(solution)/shard_map/ppermute | solution.py:22
  391.7 7.9 %copy-start = (f32[32,4]{0,1:T(4,128)S(1)}, f32[32,4]{0,1:T(4,128)}, u32[]{:S(2)}) copy-start(f32[32,4]{0,1:T(4,128)} %param.10) | copy-start | bytes 1540
  391.7 65.2 %all-to-all-start.3 = ((bf16[32,24,2880]{2,1,0:T(8,128)(2,1)}), bf16[32,24,2880]{2,1,0:T(8,128)(2,1)}, u32[]{:S(2)}, u32[]{:S(2)}) async-start(bf16[32,24,2880]{2,1,0:T(8,128)(2,1)} %bitcast.69), calls=%async_computation.3 | async-start | bytes 9043968 | tf_op jit(solution)/shard_map/all_to_all | solution.py:147
Sparse Core Ops, SparseCore 0:
  143.2 92.3 all-reduce.3
